TPU v7x, 256 devices: a whole 4x4x8 slice. The times are simulated.
256 devices in a mesh: dp: 32 (over x, z), tp: 8 (over y, core).
Axes of the slice: x: 4, y: 4, z: 8, core: 2. Of those that a mesh axis runs over, the one named last changes fastest.
Arguments:
- hidden_state: bfloat16 [7168, 512], P(None, 'dp'), may hold values from -6 to 6
- attention_gain: float32 [7168], replicated, may hold values from 0.1 to 1.9
- down_weight: bfloat16 [7168, 2112], P(None, 'tp'), may hold values from -0.0625 to 0.0625
- query_gain: float32 [1536], replicated, may hold values from 0.1 to 1.9
- latent_gain: float32 [512], replicated, may hold values from 0.1 to 1.9
- query_weight: bfloat16 [128, 576, 1536], P('tp', 'dp'), may hold values from -0.15625 to 0.15625
- latent_cache: bfloat16 [256, 4096, 576], P('dp'), may hold values from -240 to 240
- cache_length: int32 [256], P('dp'), may hold values from 1 to 4096
- owner_place: int32 [256], replicated, may hold values from 0 to 255, each once
- accept_length: int32 [256], replicated, may hold values from 1 to 2
- value_weight: bfloat16 [128, 512, 128], P('tp'), may hold values from -0.25 to 0.25
- output_weight: bfloat16 [7168, 16384], P('dp', 'tp'), may hold values from -0.046875 to 0.046875
- final_gain: float32 [7168], replicated, may hold values from 0.1 to 1.9
- head_weight: bfloat16 [7168, 65536], P(None, ('dp', 'tp')), may hold values from -8 to 8
- draft_tokens: int32 [256, 2], replicated, may hold values from 0 to 65535
Outputs:
- log_probs: float32 [512, 65536], P(None, ('dp', 'tp'))
- draft_scores: float32 [512], replicated
- committed: bfloat16 [256, 2, 576], P('dp')
All inputs are finite; a program needn't handle non-finite values.
Results may differ from a plain program's by a relative error of at most 0.006.
The roundings to bfloat16 on the way count: a program that leaves them out, or rounds other values in their place, can miss the bound.
Values may be sent and summed in bfloat16 or wider, within the bound.
No kernel may reach another device: no remote copies, remote signals or barrier semaphores. Data moves between devices by JAX's collectives and lax.ppermute only.
A program may use at most 192 MiB of HBM per device.

v0:
```python
import jax
import jax.numpy as jnp
from jax import lax
from jax.sharding import PartitionSpec as P

D = 7168
QL = 1536
DL = 512
DR = 64
epsilon = 1e-06
score_scale = 192.0 ** (-0.5)
masked_score = -1e30


def row_norm(values, gain_vector):
    inverse_rms = lax.rsqrt(jnp.mean(values * values, axis=-1, keepdims=True) + epsilon)
    return values * inverse_rms * gain_vector


def round_keep(values):
    return lax.optimization_barrier(values.astype(jnp.bfloat16)).astype(jnp.float32)


def on_device(
    hidden_state,
    attention_gain,
    down_weight,
    query_gain,
    latent_gain,
    query_weight,
    latent_cache,
    cache_length,
    owner_place,
    accept_length,
    value_weight,
    output_weight,
    final_gain,
    head_weight,
    draft_tokens,
):
    dp_count = lax.axis_size("dp")
    tp_count = lax.axis_size("tp")
    dp_rank = lax.axis_index("dp")
    tp_rank = lax.axis_index("tp")
    request_count = draft_tokens.shape[0]
    step_count = draft_tokens.shape[1]
    row_count = request_count * step_count
    local_requests = latent_cache.shape[0]
    local_rows = local_requests * step_count
    context = latent_cache.shape[1]
    slice_width = query_weight.shape[1]
    local_heads = value_weight.shape[0]
    value_width = value_weight.shape[2]
    stream = hidden_state.astype(jnp.float32)
    scaled = (stream * attention_gain[:, None]).astype(jnp.bfloat16)
    column_part = lax.dot_general(
        scaled, down_weight, (((0,), (0,)), ((), ())), preferred_element_type=jnp.float32
    )
    projected = lax.all_gather(column_part, "tp", axis=1, tiled=True)
    inverse_norm = lax.rsqrt(jnp.sum(stream * stream, axis=0) / D + epsilon)
    latent = projected * inverse_norm[:, None]
    query_latent = row_norm(latent[:, :QL], query_gain).astype(jnp.bfloat16)
    latent_part = row_norm(latent[:, QL : QL + DL], latent_gain)
    fresh_rows = jnp.concatenate([latent_part, latent[:, QL + DL :]], axis=1).astype(jnp.bfloat16)
    every_query, every_fresh = (
        lax.all_gather(query_latent, "dp", axis=0, tiled=True),
        lax.all_gather(fresh_rows, "dp", axis=0, tiled=True),
    )
    query_part = lax.dot_general(
        every_query, query_weight, (((1,), (2,)), ((), ())), preferred_element_type=jnp.float32
    )
    query_part = query_part.astype(jnp.bfloat16).reshape(row_count, local_heads * slice_width)
    step_index = jnp.arange(step_count, dtype=jnp.int32)
    owner_row = (owner_place[:, None] * step_count + step_index[None, :]).reshape(row_count)
    row_index = jnp.arange(row_count, dtype=jnp.int32)
    reorder = (owner_row[None, :] == row_index[:, None]).astype(jnp.bfloat16)
    query_owned = jnp.dot(reorder, query_part, preferred_element_type=jnp.float32).astype(
        jnp.bfloat16
    )
    own_reorder = lax.dynamic_slice_in_dim(reorder, dp_rank * local_rows, local_rows, 0)
    own_fresh = jnp.dot(own_reorder, every_fresh, preferred_element_type=jnp.float32).astype(
        jnp.bfloat16
    )
    own_fresh = own_fresh.reshape(local_requests, step_count, DL + DR)
    arrived = lax.all_to_all(query_owned, "dp", split_axis=0, concat_axis=1, tiled=True)
    arrived = arrived.reshape(local_requests, step_count, dp_count, local_heads, slice_width)
    cache_blocks = latent_cache.reshape(local_requests, context, dp_count, slice_width)
    fresh_blocks = own_fresh.reshape(local_requests, step_count, dp_count, slice_width)
    old_scores = (
        jnp.einsum("usdhc,updc->ushp", arrived, cache_blocks, preferred_element_type=jnp.float32)
        * score_scale
    )
    live_mask = jnp.arange(context, dtype=jnp.int32)[None, :] < cache_length[:, None]
    old_scores = jnp.where(live_mask[:, None, None, :], old_scores, masked_score)
    new_scores = (
        jnp.einsum("usdhc,ukdc->ushk", arrived, fresh_blocks, preferred_element_type=jnp.float32)
        * score_scale
    )
    causal = step_index[None, :] <= step_index[:, None]
    new_scores = jnp.where(causal[None, :, None, :], new_scores, masked_score)
    row_peak = jnp.maximum(jnp.max(old_scores, axis=-1), jnp.max(new_scores, axis=-1))
    old_exp = jnp.exp(old_scores - row_peak[..., None])
    new_exp = jnp.exp(new_scores - row_peak[..., None])
    exp_total = jnp.sum(old_exp, axis=-1) + jnp.sum(new_exp, axis=-1)
    old_weight = (old_exp / exp_total[..., None]).astype(jnp.bfloat16)
    new_weight = (new_exp / exp_total[..., None]).astype(jnp.bfloat16)
    mixed_values = jnp.einsum(
        "ushp,upc->ushc", old_weight, latent_cache[:, :, :DL], preferred_element_type=jnp.float32
    )
    mixed_values = mixed_values + jnp.einsum(
        "ushk,ukc->ushc", new_weight, own_fresh[:, :, :DL], preferred_element_type=jnp.float32
    )
    attended = mixed_values.astype(jnp.bfloat16)
    head_values = jnp.einsum(
        "ushc,hcv->ushv", attended, value_weight, preferred_element_type=jnp.float32
    )
    head_values = head_values.astype(jnp.bfloat16).reshape(local_rows, local_heads * value_width)
    slot_terms = lax.dot_general(
        output_weight,
        lax.all_gather(head_values, "dp", axis=0, tiled=True),
        (((1,), (1,)), ((), ())),
        preferred_element_type=jnp.float32,
    )
    request_terms = jnp.take(slot_terms, owner_row, axis=1)
    block_sum = lax.psum(request_terms, "tp")
    attn_output = lax.all_to_all(
        block_sum.astype(jnp.bfloat16), "dp", split_axis=1, concat_axis=0, tiled=True
    ).astype(block_sum.dtype)
    residual = round_keep(stream + attn_output)
    square_total = jnp.sum(residual * residual, axis=0)
    normed = residual * lax.rsqrt(square_total / D + epsilon)[None, :] * final_gain[:, None]
    normed = normed.astype(jnp.bfloat16)
    whole_normed = lax.all_gather(normed, "dp", axis=1, tiled=True)
    logits = lax.dot_general(
        whole_normed, head_weight, (((0,), (0,)), ((), ())), preferred_element_type=jnp.float32
    )
    vocab_width = head_weight.shape[1]
    vocab_start = (dp_rank * tp_count + tp_rank) * vocab_width
    draft_flat = draft_tokens.reshape(row_count)
    target_hit = (draft_flat - vocab_start)[:, None] == jnp.arange(vocab_width, dtype=jnp.int32)[
        None, :
    ]
    target_part = jnp.sum(jnp.where(target_hit, logits, jnp.zeros_like(logits)), axis=1)
    local_peak = jnp.max(logits, axis=1)
    vocab_peak = lax.pmax(local_peak, ("dp", "tp"))
    shifted_total = jnp.sum(jnp.exp(logits - vocab_peak[:, None]), axis=1)
    vocab_total, target = lax.psum((shifted_total, target_part), ("dp", "tp"))
    log_total = vocab_peak + jnp.log(vocab_total)
    accepted = (step_index[None, :] < accept_length[:, None]).reshape(row_count)
    log_probs = jnp.where(accepted[:, None], logits - log_total[:, None], jnp.zeros_like(logits))
    draft_scores = jnp.where(accepted, target - log_total, jnp.zeros_like(target))
    slot_global = dp_rank * local_requests + jnp.arange(local_requests, dtype=jnp.int32)
    slot_match = owner_place[None, :] == slot_global[:, None]
    slot_accept = jnp.sum(
        jnp.where(slot_match, accept_length[None, :], jnp.zeros_like(slot_match, dtype=jnp.int32)),
        axis=1,
    )
    keep_mask = step_index[None, :, None] < slot_accept[:, None, None]
    committed = jnp.where(keep_mask, own_fresh, jnp.zeros_like(own_fresh))
    return (log_probs, draft_scores, committed)


def solution(mesh):
    return jax.shard_map(
        on_device,
        mesh=mesh,
        in_specs=(
            P(None, "dp"),
            P(),
            P(None, "tp"),
            P(),
            P(),
            P("tp", "dp", None),
            P("dp", None, None),
            P("dp"),
            P(),
            P(),
            P("tp", None, None),
            P("dp", "tp"),
            P(),
            P(None, ("dp", "tp")),
            P(),
        ),
        out_specs=(P(None, ("dp", "tp")), P(), P("dp", None, None)),
        check_vma=False,
    )
```

profile of v0, /device:TPU:1, one launch (start us, length us, event | category | flops | bytes accessed | tf_op | source)
XLA Modules:
  0.0 611.3 jit_solution(11450530921332447881)
XLA Ops:
  7.3 1.2 fusion.38
  8.5 3.4 convolution_bitcast_fusion.1
  11.9 15.8 %all-gather = f32[8,264,16]{1,2,0:T(8,128)S(1)} all-gather(f32[1,264,16]{1,2,0:T(8,128)S(1)} %convolution_bitcast_fusion.1), channel_id=1, replica_groups=mesh['dp'=32,'tp'=8] {'tp'}, dimensions={0}, use_global_device_ids=true | all-gather | bytes 152064 | tf_op jit(solution)/shard_map/all_gather | solution.py:59
  28.1 0.7 multiply_convert_fusion
  29.4 40.8 %all_gather.17 = bf16[512,576]{1,0:T(8,128)(2,1)S(1)} all-gather(bf16[16,576]{1,0:T(8,128)(2,1)S(1)} %pad_maximum_fusion), channel_id=1, replica_groups=mesh['dp'=32,'tp'=8] {'dp'}, dimensions={0}, use_global_device_ids=true | all-gather | bytes 608256 | tf_op jit(solution)/shard_map/all_gather | solution.py:67
  71.1 32.7 %copy.58 = bf16[8,4096,576]{1,0,2:T(8,128)(2,1)} copy(bf16[8,4096,576]{1,2,0:T(8,128)(2,1)} %param.21) | data formatting | bytes 75497472 | tf_op args[6]
  103.9 2.5 fusion.19
  106.5 0.4 convolution_convert_fusion
  106.9 0.9 copy.56
  107.8 6.1 all-to-all-start
  114.1 10.1 %all-to-all-done = bf16[32,16,288]{2,1,0:T(8,128)(2,1)S(1)} async-done(((bf16[32,16,288]{2,1,0:T(8,128)(2,1)}), bf16[32,16,288]{2,1,0:T(8,128)(2,1)S(1)}, u32[]{:S(2)}, u32[]{:S(2)}) %all-to-all-start) | async-done | bytes 294944 | tf_op jit(solution)/shard_map/all_to_all | solution.py:85
  124.2 2.2 copy.57
  126.4 2.8 fusion.50
  129.2 73.5 %fusion.8 = (f32[8,2,16]{2,1,0:T(2,128)S(1)}, f32[8,2,16,4096]{3,2,1,0:T(8,128)S(1)}) fusion(pred[8,4096]{1,0:T(8,128)(4,1)S(1)} %iota_compare_fusion.2, bf16[8,4096,32,18,1]{1,0,3,2,4:T(8,128)(2,1)} %bitcast.77, bf16[8,2,32,16,18]{2,1,0,4,3:T(2,128)(2,1)} %bitcast.80), kind=kOutput, calls=%fused_computation.10 | convolution fusion | flops 1211105024 | bytes 42271744 | tf_op jit(solution)/shard_map/usdhc,updc->ushp/dot_general | solution.py:90
  202.7 1.9 copy-done.1
  204.6 1.2 fusion.9
  205.8 15.8 %fusion.2 = f32[8,2,16,512]{3,2,1,0:T(8,128)S(1)} fusion(bf16[8,4096,576]{1,2,0:T(8,128)(2,1)} %param.21, f32[8,2,16,4096]{3,2,1,0:T(8,128)} %copy-done.1, f32[8,2,16]{2,1,0:T(2,128)S(1)} %add.129, f32[8,2,16]{2,1,0:T(2,128)S(1)} %max.9, pred[8,4096]{1,0:T(8,128)(4,1)S(1)} %iota_compare_fusion.2), kind=kOutput, calls=%fused_computation.3 | convolution fusion | flops 1078984704 | bytes 38307840 | tf_op jit(solution)/shard_map/ushp,upc->ushc/dot_general | solution.py:107
  221.9 0.5 fusion.27
  222.3 0.6 copy.102
  223.2 81.2 %all-gather.7.cloned.1.call-done = bf16[512,2048]{1,0:T(8,128)(2,1)} async-done(((bf16[16,2048]{1,0:T(8,128)(2,1)}), bf16[512,2048]{1,0:T(8,128)(2,1)}) %all-gather.7.cloned.1.call-update) | async-done | bytes 2097168 | tf_op jit(solution)/shard_map/all_gather | solution.py:120
  304.5 2.6 convolution_bitcast_fusion
  307.3 1.6 gather_fusion
  309.1 30.8 %all-reduce.2 = bf16[224,512]{0,1:T(8,128)(2,1)S(1)} all-reduce(f32[224,512]{0,1:T(8,128)S(1)} %select_bitcast_fusion), channel_id=1, replica_groups=mesh['dp'=32,'tp'=8] {'tp'}, use_global_device_ids=true, to_apply=%region_7.8 | all-reduce | flops 114688 | bytes 688128 | tf_op jit(solution)/shard_map/psum | solution.py:125
  339.9 14.9 %all_to_all.29 = bf16[224,32,16]{0,2,1:T(8,128)(2,1)S(1)} all-to-all(bf16[224,32,16]{0,2,1:T(8,128)(2,1)S(1)} %bitcast.81), channel_id=1, replica_groups=mesh['dp'=32,'tp'=8] {'dp'}, dimensions={1} | all-to-all | bytes 458752 | tf_op jit(solution)/shard_map/all_to_all | solution.py:126
  355.8 0.8 fusion.36
  357.4 0.7 broadcast_select_fusion
  358.1 90.3 %all-gather.9.cloned.1.call-done = bf16[7168,512]{0,1:T(8,128)(2,1)} async-done(((bf16[7168,16]{0,1:T(8,128)(2,1)}), bf16[7168,512]{0,1:T(8,128)(2,1)}) %all-gather.9.cloned.1.call-update) | async-done | bytes 7340048 | tf_op jit(solution)/shard_map/all_gather | solution.py:133
  448.5 6.2 %fusion.51 = (f32[512]{0:T(512)S(1)}, f32[512,256]{0,1:T(8,128)S(1)}) fusion(bf16[7168,512]{0,1:T(8,128)(2,1)} %all-gather.9.cloned.1.call-done, bf16[7168,256]{1,0:T(8,128)(2,1)} %param.28), kind=kOutput, calls=%fused_computation.95 | convolution fusion | flops 1879178752 | bytes 11536384 | tf_op jit(solution)/shard_map/dot_general | solution.py:134
  454.7 75.1 %pmax.7 = f32[512]{0:T(512)S(1)} all-reduce(f32[512]{0:T(512)S(1)} %get-tuple-element.25), channel_id=1, replica_groups=mesh['dp'=32,'tp'=8] {'dp','tp'}, use_global_device_ids=true, to_apply=%region_10.11 | all-reduce | flops 512 | bytes 4096 | tf_op jit(solution)/shard_map/pmax | solution.py:145
  529.9 72.8 %all-reduce = (f32[512]{0:T(512)S(1)}, f32[512]{0:T(512)S(1)}) all-reduce(f32[512]{0:T(512)S(1)} %get-tuple-element.16, f32[512]{0:T(512)S(1)} %get-tuple-element.15), channel_id=1, replica_groups=mesh['dp'=32,'tp'=8] {'dp','tp'}, use_global_device_ids=true, to_apply=%region_12.13 | all-reduce | flops 1024 | bytes 8192 | tf_op jit(solution)/shard_map/psum | solution.py:147
  602.7 0.6 subtract_select_fusion.1
  603.4 1.0 copy.69
  (75 shorter events, 4.9 us)
Async XLA Ops:
  7.2 214.7 %copy-start = (bf16[16,512,128]{2,1,0:T(8,128)(2,1)S(1)}, bf16[16,512,128]{2,1,0:T(8,128)(2,1)}, u32[]{:S(2)}) copy-start(bf16[16,512,128]{2,1,0:T(8,128)(2,1)} %param.25) | copy-start | bytes 6291460
  7.2 21.0 %copy-start.4 = (f32[1536]{0:T(1024)S(1)}, f32[1536]{0:T(1024)}, u32[]{:S(2)}) copy-start(f32[1536]{0:T(1024)} %param.18) | copy-start | bytes 18436
  7.2 21.7 %copy-start.6 = (s32[256]{0:T(256)S(1)}, s32[256]{0:T(256)}, u32[]{:S(2)}) copy-start(s32[256]{0:T(256)} %param.23) | copy-start | bytes 3076
  7.2 22.1 %copy-start.7 = (f32[512]{0:T(512)S(1)}, f32[512]{0:T(512)}, u32[]{:S(2)}) copy-start(f32[512]{0:T(512)} %param.19) | copy-start | bytes 6148
  7.2 96.6 %all-gather.5.cloned.1.call-start = ((), (), s32[]{:S(2)}) async-start(), calls=%async_computation.2 | async-start | bytes 1622016 | tf_op jit(solution)/shard_map/all_gather | solution.py:66
  103.8 10.2 %copy-start.9 = (s32[8]{0:T(128)S(1)}, s32[8]{0:T(128)}, u32[]{:S(2)}) copy-start(s32[8]{0:T(128)} %param.22) | copy-start | bytes 100
  107.8 16.4 %all-to-all-start = ((bf16[32,16,288]{2,1,0:T(8,128)(2,1)}), bf16[32,16,288]{2,1,0:T(8,128)(2,1)S(1)}, u32[]{:S(2)}, u32[]{:S(2)}) async-start(bf16[32,16,288]{2,1,0:T(8,128)(2,1)} %bitcast.4), calls=%async_computation | async-start | bytes 786432 | tf_op jit(solution)/shard_map/all_to_all | solution.py:85
  113.9 190.5 %all-gather.7.cloned.1.call-start = ((), (), s32[]{:S(2)}) async-start(), calls=%async_computation.3 | async-start | bytes 2162688 | tf_op jit(solution)/shard_map/all_gather | solution.py:120
  202.6 1.9 copy-start.1
  223.0 225.5 %all-gather.9.cloned.1.call-start = ((), (), s32[]{:S(2)}) async-start(), calls=%async_computation.4 | async-start | bytes 7569408 | tf_op jit(solution)/shard_map/all_gather | solution.py:133
  307.3 48.2 %copy-start.2 = (bf16[7168,16]{0,1:T(8,128)(2,1)S(1)}, bf16[7168,16]{0,1:T(8,128)(2,1)}, u32[]{:S(2)}) copy-start(bf16[7168,16]{0,1:T(8,128)(2,1)} %param.15) | copy-start | bytes 688132
  308.9 46.8 %copy-start.3 = (f32[7168]{0:T(1024)S(1)}, f32[7168]{0:T(1024)}, u32[]{:S(2)}) copy-start(f32[7168]{0:T(1024)} %param.27) | copy-start | bytes 86020
  308.9 47.7 %copy-start.5 = (s32[256]{0:T(256)S(1)}, s32[256]{0:T(256)}, u32[]{:S(2)}) copy-start(s32[256]{0:T(256)} %param.24) | copy-start | bytes 3076
  308.9 47.9 %copy-start.8 = (s32[256,2]{0,1:T(2,128)S(1)}, s32[256,2]{0,1:T(2,128)}, u32[]{:S(2)}) copy-start(s32[256,2]{0,1:T(2,128)} %param.29) | copy-start | bytes 6148
Sparse Core Ops, SparseCore 0:
  29.0 73.0 all-gather.4
  223.1 81.3 all-gather.6
  356.7 91.7 all-gather.8
where the time goes:
time: 618 us; the launch traced here: 611 us
  blocking collectives  250 us (40%)
  waiting for transfers between devices  182 us (29%)
  matrix products  108 us (17%)
  local copies, waits for them, and re-layouts  43.3 us (7%)
  between operations  14.6 us (2%)
  other arithmetic  7.1 us (1%)
  starting transfers between devices  6.22 us (1%)
    all_gather x1, waiting for transfers between devices, on_device(): whole_normed = lax.all_gather(normed, 'dp', axis=1, tiled=True)  90.3 us
    all_gather x1, waiting for transfers between devices, on_device(): lax.all_gather(head_values, 'dp', axis=0, tiled=True)  81.2 us
    pmax x1, blocking collectives, on_device(): vocab_peak = lax.pmax(local_peak, ('dp', 'tp'))  75.1 us
    dot_general x1, matrix products, on_device(): jnp.einsum('usdhc,updc->ushp', arrived, cache_blocks, preferred_element_t...  73.5 us
    psum x1, blocking collectives, on_device(): vocab_total, target = lax.psum((shifted_total, target_part), ('dp', 'tp'))  72.8 us
    all_gather x1, blocking collectives, on_device(): lax.all_gather(fresh_rows, 'dp', axis=0, tiled=True)  40.8 us
    unnamed x24, local copies, waits for them, and re-layouts  36.4 us
    psum x1, blocking collectives, on_device(): block_sum = lax.psum(request_terms, 'tp')  30.8 us
  transfers between devices with their start and end apart: 4, of which 3 were waited for; matrix products, arithmetic and copies ran while one was open for 6% of the time, Pallas kernels for 0%

commit v1 on v0

--- a/solution.py
+++ b/solution.py
@@ -10,6 +10,11 @@
 epsilon = 1e-06
 score_scale = 192.0 ** (-0.5)
 masked_score = -1e30
+
+
+def exchange_gather(x, mesh_axis, dim):
+    sent = jnp.stack([x] * lax.axis_size(mesh_axis))
+    return jnp.concatenate(lax.all_to_all(sent, mesh_axis, 0, 0), axis=dim)
 
 
 def row_norm(values, gain_vector):
@@ -64,7 +69,7 @@
     fresh_rows = jnp.concatenate([latent_part, latent[:, QL + DL :]], axis=1).astype(jnp.bfloat16)
     every_query, every_fresh = (
         lax.all_gather(query_latent, "dp", axis=0, tiled=True),
-        lax.all_gather(fresh_rows, "dp", axis=0, tiled=True),
+        exchange_gather(fresh_rows, "dp", 0),
     )
     query_part = lax.dot_general(
         every_query, query_weight, (((1,), (2,)), ((), ())), preferred_element_type=jnp.float32

time: 618 us -> 611 us (0.989)
  blocking collectives: 250 us -> 209 us
  waiting for transfers between devices: 182 us -> 205 us
  starting transfers between devices: 6.22 us -> 15.5 us
    all_gather x1 -> x0, blocking collectives: 40.8 us -> none  [on_device(): lax.all_gather(fresh_rows, 'dp', axis=0, tiled=True)]
    all_gather x1, waiting for transfers between devices: 0.02 us -> 29.5 us  [on_device(): lax.all_gather(query_latent, 'dp', axis=0, tiled=True)]
    all_to_all x0 -> x1, starting transfers between devices: none -> 9.84 us  [exchange_gather(): return jnp.concatenate(lax.all_to_all(sent, mesh_axis, 0, 0), axis=dim)]
  transfers between devices with their start and end apart: 4 -> 5, of which waited for: 3 -> 4; matrix products, arithmetic and copies ran while one was open for 6% -> 7% of each run, Pallas kernels for 0% -> 0%
where the time goes in v1:
time: 611 us; the launch traced here: 604 us
  blocking collectives  209 us (34%)
  waiting for transfers between devices  205 us (34%)
  matrix products  107 us (18%)
  local copies, waits for them, and re-layouts  44.9 us (7%)
  starting transfers between devices  15.5 us (3%)
  between operations  14.2 us (2%)
  other arithmetic  7.1 us (1%)
    all_gather x1, waiting for transfers between devices, on_device(): whole_normed = lax.all_gather(normed, 'dp', axis=1, tiled=True)  90.3 us
    all_gather x1, waiting for transfers between devices, on_device(): lax.all_gather(head_values, 'dp', axis=0, tiled=True)  76.2 us
    pmax x1, blocking collectives, on_device(): vocab_peak = lax.pmax(local_peak, ('dp', 'tp'))  75.1 us
    psum x1, blocking collectives, on_device(): vocab_total, target = lax.psum((shifted_total, target_part), ('dp', 'tp'))  72.8 us
    dot_general x1, matrix products, on_device(): jnp.einsum('usdhc,updc->ushp', arrived, cache_blocks, preferred_element_t...  71.6 us
    unnamed x24, local copies, waits for them, and re-layouts  36.4 us
    psum x1, blocking collectives, on_device(): block_sum = lax.psum(request_terms, 'tp')  30.8 us
    all_gather x1, waiting for transfers between devices, on_device(): lax.all_gather(query_latent, 'dp', axis=0, tiled=True)  29.5 us
  transfers between devices with their start and end apart: 5, of which 4 were waited for; matrix products, arithmetic and copies ran while one was open for 7% of the time, Pallas kernels for 0%

profile of v1, /device:TPU:1, one launch (start us, length us, event | category | flops | bytes accessed | tf_op | source)
XLA Modules:
  0.0 603.9 jit_solution(6321121302445125948)
XLA Ops:
  7.3 1.2 fusion.38
  8.5 3.4 convolution_bitcast_fusion.1
  11.9 15.8 %all-gather = f32[8,264,16]{1,2,0:T(8,128)S(1)} all-gather(f32[1,264,16]{1,2,0:T(8,128)S(1)} %convolution_bitcast_fusion.1), channel_id=1, replica_groups=mesh['dp'=32,'tp'=8] {'tp'}, dimensions={0}, use_global_device_ids=true | all-gather | bytes 152064 | tf_op jit(solution)/shard_map/all_gather | solution.py:64
  28.2 0.7 multiply_convert_fusion
  29.1 0.9 stack.2
  30.0 9.8 %all-to-all-start.1 = ((bf16[32,16,576]{2,1,0:T(8,128)(2,1)}), bf16[32,16,576]{2,1,0:T(8,128)(2,1)S(1)}, u32[]{:S(2)}, u32[]{:S(2)}) async-start(bf16[32,16,576]{2,1,0:T(8,128)(2,1)} %stack.2), calls=%async_computation.1 | async-start | bytes 1310720 | tf_op jit(solution)/shard_map/all_to_all | solution.py:17
  40.2 32.8 %copy.58 = bf16[8,4096,576]{1,0,2:T(8,128)(2,1)} copy(bf16[8,4096,576]{1,2,0:T(8,128)(2,1)} %param.21) | data formatting | bytes 75497472 | tf_op args[6]
  73.0 29.5 %all-gather.5.cloned.1.call-done = bf16[512,1536]{1,0:T(8,128)(2,1)} async-done(((bf16[16,1536]{1,0:T(8,128)(2,1)}), bf16[512,1536]{1,0:T(8,128)(2,1)}) %all-gather.5.cloned.1.call-update) | async-done | bytes 1572880 | tf_op jit(solution)/shard_map/all_gather | solution.py:71
  102.5 2.6 fusion.19
  105.1 0.8 reshape.222
  105.9 1.3 convolution_convert_fusion
  107.2 0.9 copy.56
  108.1 5.6 all-to-all-start
  114.7 9.3 %all-to-all-done = bf16[32,16,288]{2,1,0:T(8,128)(2,1)S(1)} async-done(((bf16[32,16,288]{2,1,0:T(8,128)(2,1)}), bf16[32,16,288]{2,1,0:T(8,128)(2,1)S(1)}, u32[]{:S(2)}, u32[]{:S(2)}) %all-to-all-start) | async-done | bytes 294944 | tf_op jit(solution)/shard_map/all_to_all | solution.py:90
  124.0 2.2 copy.57
  126.2 2.8 fusion.50
  128.9 71.6 %fusion.8 = (f32[8,2,16]{2,1,0:T(2,128)S(1)}, f32[8,2,16,4096]{3,2,1,0:T(8,128)S(1)}) fusion(pred[8,4096]{1,0:T(8,128)(4,1)S(1)} %iota_compare_fusion.2, bf16[8,4096,32,18,1]{1,0,3,2,4:T(8,128)(2,1)} %bitcast.78, bf16[8,2,32,16,18]{2,1,0,4,3:T(2,128)(2,1)} %bitcast.82), kind=kOutput, calls=%fused_computation.10 | convolution fusion | flops 1211105024 | bytes 42271744 | tf_op jit(solution)/shard_map/usdhc,updc->ushp/dot_general | solution.py:95
  200.7 1.9 copy-done.1
  202.5 1.2 fusion.9
  203.7 15.8 %fusion.2 = f32[8,2,16,512]{3,2,1,0:T(8,128)S(1)} fusion(bf16[8,4096,576]{1,2,0:T(8,128)(2,1)} %param.21, f32[8,2,16,4096]{3,2,1,0:T(8,128)} %copy-done.1, f32[8,2,16]{2,1,0:T(2,128)S(1)} %add.129, f32[8,2,16]{2,1,0:T(2,128)S(1)} %max.9, pred[8,4096]{1,0:T(8,128)(4,1)S(1)} %iota_compare_fusion.2), kind=kOutput, calls=%fused_computation.3 | convolution fusion | flops 1078984704 | bytes 38307840 | tf_op jit(solution)/shard_map/ushp,upc->ushc/dot_general | solution.py:112
  221.2 76.2 %all-gather.7.cloned.1.call-done = bf16[512,2048]{1,0:T(8,128)(2,1)} async-done(((bf16[16,2048]{1,0:T(8,128)(2,1)}), bf16[512,2048]{1,0:T(8,128)(2,1)}) %all-gather.7.cloned.1.call-update) | async-done | bytes 2097168 | tf_op jit(solution)/shard_map/all_gather | solution.py:125
  297.5 2.6 convolution_bitcast_fusion
  300.3 1.6 gather_fusion
  302.1 30.8 %all-reduce.2 = bf16[224,512]{0,1:T(8,128)(2,1)S(1)} all-reduce(f32[224,512]{0,1:T(8,128)S(1)} %select_bitcast_fusion), channel_id=1, replica_groups=mesh['dp'=32,'tp'=8] {'tp'}, use_global_device_ids=true, to_apply=%region_7.8 | all-reduce | flops 114688 | bytes 688128 | tf_op jit(solution)/shard_map/psum | solution.py:130
  332.9 14.9 %all_to_all.34 = bf16[224,32,16]{0,2,1:T(8,128)(2,1)S(1)} all-to-all(bf16[224,32,16]{0,2,1:T(8,128)(2,1)S(1)} %bitcast.83), channel_id=1, replica_groups=mesh['dp'=32,'tp'=8] {'dp'}, dimensions={1} | all-to-all | bytes 458752 | tf_op jit(solution)/shard_map/all_to_all | solution.py:131
  348.7 0.8 fusion.36
  350.4 0.7 broadcast_select_fusion
  351.1 90.3 %all-gather.9.cloned.1.call-done = bf16[7168,512]{0,1:T(8,128)(2,1)} async-done(((bf16[7168,16]{0,1:T(8,128)(2,1)}), bf16[7168,512]{0,1:T(8,128)(2,1)}) %all-gather.9.cloned.1.call-update) | async-done | bytes 7340048 | tf_op jit(solution)/shard_map/all_gather | solution.py:138
  441.5 6.2 %fusion.51 = (f32[512]{0:T(512)S(1)}, f32[512,256]{0,1:T(8,128)S(1)}) fusion(bf16[7168,512]{0,1:T(8,128)(2,1)} %all-gather.9.cloned.1.call-done, bf16[7168,256]{1,0:T(8,128)(2,1)} %param.28), kind=kOutput, calls=%fused_computation.95 | convolution fusion | flops 1879178752 | bytes 11536384 | tf_op jit(solution)/shard_map/dot_general | solution.py:139
  447.7 75.1 %pmax.7 = f32[512]{0:T(512)S(1)} all-reduce(f32[512]{0:T(512)S(1)} %get-tuple-element.25), channel_id=1, replica_groups=mesh['dp'=32,'tp'=8] {'dp','tp'}, use_global_device_ids=true, to_apply=%region_10.11 | all-reduce | flops 512 | bytes 4096 | tf_op jit(solution)/shard_map/pmax | solution.py:150
  522.9 72.8 %all-reduce = (f32[512]{0:T(512)S(1)}, f32[512]{0:T(512)S(1)}) all-reduce(f32[512]{0:T(512)S(1)} %get-tuple-element.16, f32[512]{0:T(512)S(1)} %get-tuple-element.15), channel_id=1, replica_groups=mesh['dp'=32,'tp'=8] {'dp','tp'}, use_global_device_ids=true, to_apply=%region_12.13 | all-reduce | flops 1024 | bytes 8192 | tf_op jit(solution)/shard_map/psum | solution.py:152
  596.4 1.0 copy.69
  (77 shorter events, 6.5 us)
Async XLA Ops:
  7.2 212.7 %copy-start = (bf16[16,512,128]{2,1,0:T(8,128)(2,1)S(1)}, bf16[16,512,128]{2,1,0:T(8,128)(2,1)}, u32[]{:S(2)}) copy-start(bf16[16,512,128]{2,1,0:T(8,128)(2,1)} %param.25) | copy-start | bytes 6291460
  7.2 21.0 %copy-start.4 = (f32[1536]{0:T(1024)S(1)}, f32[1536]{0:T(1024)}, u32[]{:S(2)}) copy-start(f32[1536]{0:T(1024)} %param.18) | copy-start | bytes 18436
  7.2 21.8 %copy-start.7 = (f32[512]{0:T(512)S(1)}, f32[512]{0:T(512)}, u32[]{:S(2)}) copy-start(f32[512]{0:T(512)} %param.19) | copy-start | bytes 6148
  7.2 32.6 %copy-start.9 = (s32[8]{0:T(128)S(1)}, s32[8]{0:T(128)}, u32[]{:S(2)}) copy-start(s32[8]{0:T(128)} %param.22) | copy-start | bytes 100
  7.2 32.7 %copy-start.6 = (s32[256]{0:T(256)S(1)}, s32[256]{0:T(256)}, u32[]{:S(2)}) copy-start(s32[256]{0:T(256)} %param.23) | copy-start | bytes 3076
  7.2 95.3 %all-gather.5.cloned.1.call-start = ((), (), s32[]{:S(2)}) async-start(), calls=%async_computation.3 | async-start | bytes 1622016 | tf_op jit(solution)/shard_map/all_gather | solution.py:71
  30.0 78.1 %all-to-all-start.1 = ((bf16[32,16,576]{2,1,0:T(8,128)(2,1)}), bf16[32,16,576]{2,1,0:T(8,128)(2,1)S(1)}, u32[]{:S(2)}, u32[]{:S(2)}) async-start(bf16[32,16,576]{2,1,0:T(8,128)(2,1)} %stack.2), calls=%async_computation.1 | async-start | bytes 1310720 | tf_op jit(solution)/shard_map/all_to_all | solution.py:17
  108.1 15.8 %all-to-all-start = ((bf16[32,16,288]{2,1,0:T(8,128)(2,1)}), bf16[32,16,288]{2,1,0:T(8,128)(2,1)S(1)}, u32[]{:S(2)}, u32[]{:S(2)}) async-start(bf16[32,16,288]{2,1,0:T(8,128)(2,1)} %bitcast.4), calls=%async_computation | async-start | bytes 786432 | tf_op jit(solution)/shard_map/all_to_all | solution.py:90
  113.7 183.8 %all-gather.7.cloned.1.call-start = ((), (), s32[]{:S(2)}) async-start(), calls=%async_computation.4 | async-start | bytes 2162688 | tf_op jit(solution)/shard_map/all_gather | solution.py:125
  200.6 1.9 copy-start.1
  221.0 220.5 %all-gather.9.cloned.1.call-start = ((), (), s32[]{:S(2)}) async-start(), calls=%async_computation.5 | async-start | bytes 7569408 | tf_op jit(solution)/shard_map/all_gather | solution.py:138
  300.3 48.2 %copy-start.2 = (bf16[7168,16]{0,1:T(8,128)(2,1)S(1)}, bf16[7168,16]{0,1:T(8,128)(2,1)}, u32[]{:S(2)}) copy-start(bf16[7168,16]{0,1:T(8,128)(2,1)} %param.15) | copy-start | bytes 688132
  301.9 46.8 %copy-start.3 = (f32[7168]{0:T(1024)S(1)}, f32[7168]{0:T(1024)}, u32[]{:S(2)}) copy-start(f32[7168]{0:T(1024)} %param.27) | copy-start | bytes 86020
  301.9 47.7 %copy-start.5 = (s32[256]{0:T(256)S(1)}, s32[256]{0:T(256)}, u32[]{:S(2)}) copy-start(s32[256]{0:T(256)} %param.24) | copy-start | bytes 3076
  301.9 47.9 %copy-start.8 = (s32[256,2]{0,1:T(2,128)S(1)}, s32[256,2]{0,1:T(2,128)}, u32[]{:S(2)}) copy-start(s32[256,2]{0,1:T(2,128)} %param.29) | copy-start | bytes 6148
Sparse Core Ops, SparseCore 0:
  29.0 73.4 all-gather.4
  221.1 76.3 all-gather.6
  349.7 91.7 all-gather.8
